TPU v7x, 32 devices: a whole 2x2x4 slice. The times are simulated.
32 devices in a mesh: gx: 16 (over z, y, x), gy: 2 (over core).
Axes of the slice: x: 2, y: 2, z: 4, core: 2. Of those that a mesh axis runs over, the one named last changes fastest.
Arguments:
- fields: bfloat16 [4, 1, 3072, 3072], P(None, None, 'gx', 'gy'), may hold values from -6 to 6
- x_codes: int32 [1024], replicated, may hold values from 0 to 1024, as said below
- y_codes: int32 [1020], replicated, may hold values from 0 to 1024, as said below
Outputs:
- spectrum: float32 [4, 1, 1024, 1020], P(None, None, 'gx', 'gy')
- lowpass: float32 [4, 1, 3072, 3072], P(None, None, 'gx', 'gy')
Inputs may be any that keep to these rules, and one draw needn't show every extreme that they name: `x_codes`: distinct codes in rising order, each naming one real Fourier basis function with wavenumber at most 512. `y_codes`: distinct codes in rising order, each naming one real Fourier basis function with wavenumber at most 512.
All inputs are finite; a program needn't handle non-finite values.
Results may differ from a plain program's by a relative error of at most 0.006.
Values may be sent and summed in bfloat16 or wider, within the bound.
A program may use at most 64 MiB of HBM per device.

v0:
```python
import functools
import math

import jax
import jax.numpy as jnp
from jax import lax
from jax.experimental import pallas as pl
from jax.experimental.pallas import tpu as pltpu
from jax.sharding import PartitionSpec as P

NX = 3072
NY = 3072
BAND = 512


def angle(freq, position, length):
    phase = freq[None, :] * position[:, None] % length
    return phase.astype(jnp.float32) * (2.0 * math.pi / length)


def mode_parts(picked, first, amount, length, live=None):
    step = 64 if amount % 64 == 0 else 8
    freq = jnp.where(picked <= BAND, picked, picked - BAND)
    coarse_angle = angle(freq, first + step * jnp.arange(amount // step, dtype=jnp.int32), length)
    fine_angle = angle(freq, jnp.arange(step, dtype=jnp.int32), length)
    norm = jnp.where(picked == 0, 1.0 / math.sqrt(length), math.sqrt(2.0 / length)).astype(jnp.float32)
    if live is not None:
        norm = jnp.where(live, norm, 0.0)
    is_cos = (picked <= BAND)[None, :]
    c, s = jnp.cos(coarse_angle), jnp.sin(coarse_angle)
    first_part = jnp.where(is_cos, c, s) * norm[None, :]
    second_part = jnp.where(is_cos, -s, c) * norm[None, :]
    fc, fs = jnp.cos(fine_angle), jnp.sin(fine_angle)
    return lax.optimization_barrier((first_part, second_part, fc, fs))


def mode_table(picked, first, amount, length, live=None):
    first_part, second_part, fc, fs = mode_parts(picked, first, amount, length, live)
    table = first_part[:, None, :] * fc[None] + second_part[:, None, :] * fs[None]
    return table.astype(jnp.bfloat16).reshape(amount, picked.shape[0])


def al(v, m):
    return pl.multiple_of(v, m)


def exchange_kernel(
    gx, lead, x_local, kx, kpad, cols,
    grid_ref, y_ref, xa_ref, xb_ref, fc_ref, fs_ref, spec_ref, wide_ref,
    other, inc, part, lines, xt, acc, coarse, syn,
    gs, gr, s1, r1, s2, r2, s3, r3, s4, r4,
):
    me = lax.axis_index("gx")
    half = lax.axis_index("gy")
    peer = 1 - half
    groups = gx // lead
    my_group, my_lead = me // lead, lax.rem(me, lead)
    bf, f32 = jnp.bfloat16, jnp.float32

    barrier = pltpu.get_barrier_semaphore()
    pl.semaphore_signal(barrier, inc=1, device_id={"gy": peer})

    @pl.loop(1, gx)
    def _(t):
        pl.semaphore_signal(barrier, inc=1, device_id={"gx": lax.rem(me + t, gx)})

    def frows(f):
        return pl.ds(al(f * x_local, x_local), x_local)

    def blk(j):
        return pl.ds(al(j * x_local, x_local), x_local)

    def lanes(base, g):
        return pl.ds(al(base + g * cols, cols), cols)

    @pl.loop(0, lead)
    def _(t):
        f = lax.rem(my_lead + t, lead)
        other[frows(f), :] = jnp.dot(
            grid_ref[frows(f), :], y_ref[:, pl.ds(al(peer * kpad, kpad), kpad)], preferred_element_type=f32
        ).astype(bf)

    pl.semaphore_wait(barrier, gx)

    def swap(f):
        return pltpu.make_async_remote_copy(
            src_ref=other.at[frows(f), :], dst_ref=inc.at[frows(f), :], send_sem=gs.at[f], recv_sem=gr.at[f],
            device_id={"gy": peer})

    @pl.loop(0, lead)
    def _(t):
        swap(lax.rem(my_lead + t, lead)).start()

    def out1(j):
        f, g = lax.rem(j, lead), j // lead
        return pltpu.make_async_remote_copy(
            src_ref=part.at[frows(f), lanes(0, g)], dst_ref=lines.at[blk(me), :], send_sem=s1.at[j],
            recv_sem=r1.at[me], device_id={"gx": j})

    def in1(j):
        return pltpu.make_async_remote_copy(
            src_ref=part.at[frows(0), lanes(0, 0)], dst_ref=lines.at[blk(j), :], send_sem=s1.at[j],
            recv_sem=r1.at[j], device_id={"gx": j})

    @pl.loop(0, lead)
    def _(t):
        f = lax.rem(my_lead + t, lead)
        own = jnp.dot(
            grid_ref[frows(f), :], y_ref[:, pl.ds(al(half * kpad, kpad), kpad)], preferred_element_type=f32
        )
        swap(f).wait_recv()
        part[frows(f), :] = (own + inc[frows(f), :].astype(f32)).astype(bf)

        @pl.loop(0, groups)
        def _(u):
            g = lax.rem(my_group + u, groups)
            j = g * lead + f

            @pl.when(j != me)
            def _():
                out1(j).start()

    lines[blk(me), :] = part[frows(my_lead), lanes(0, my_group)]

    step = fc_ref.shape[0]

    @pl.loop(0, xa_ref.shape[0])
    def _(h):
        xt[pl.ds(al(h * step, step), step), :] = (
            xa_ref[pl.ds(h, 1), :] * fc_ref[...] + xb_ref[pl.ds(h, 1), :] * fs_ref[...]
        ).astype(bf)

    acc[...] = jnp.zeros_like(acc)

    @pl.loop(0, gx)
    def _(t):
        f = lax.rem(my_lead + lead - t // groups, lead)
        g = lax.rem(my_group + t, groups)
        j = g * lead + f

        @pl.when(j != me)
        def _():
            in1(j).wait_recv()

        acc[...] += jnp.dot(lines[blk(j), :].T, xt[blk(j), :], preferred_element_type=f32)

    coarse[...] = acc[...].T.astype(bf)

    def out2(j):
        return pltpu.make_async_remote_copy(
            src_ref=syn.at[blk(j), :], dst_ref=wide_ref.at[frows(my_lead), lanes(half * kpad, my_group)],
            send_sem=s2.at[j], recv_sem=r2.at[me], device_id={"gx": j})

    def in2(j):
        f, g = lax.rem(j, lead), j // lead
        return pltpu.make_async_remote_copy(
            src_ref=syn.at[blk(j), :], dst_ref=wide_ref.at[frows(f), lanes(half * kpad, g)],
            send_sem=s2.at[j], recv_sem=r2.at[j], device_id={"gx": j})

    def mrows(j):
        return pl.ds(al(j * kx, kx), kx)

    def out3(j):
        return pltpu.make_async_remote_copy(
            src_ref=coarse.at[mrows(j), :], dst_ref=spec_ref.at[mrows(my_lead), lanes(0, my_group)],
            send_sem=s3.at[j], recv_sem=r3.at[me], device_id={"gx": j})

    def in3(j):
        f, g = lax.rem(j, lead), j // lead
        return pltpu.make_async_remote_copy(
            src_ref=coarse.at[mrows(j), :], dst_ref=spec_ref.at[mrows(f), lanes(0, g)],
            send_sem=s3.at[j], recv_sem=r3.at[j], device_id={"gx": j})

    def forward(j, side):
        f, g = lax.rem(j, lead), j // lead
        place = wide_ref.at[frows(f), lanes(side * kpad, g)]
        return pltpu.make_async_remote_copy(
            src_ref=place, dst_ref=place, send_sem=s4.at[j], recv_sem=r4.at[j], device_id={"gy": peer})

    @pl.loop(1, gx)
    def _(t):
        f = lax.rem(my_lead + t // groups, lead)
        g = lax.rem(my_group + t, groups)
        j = g * lead + f
        syn[blk(j), :] = jnp.dot(xt[blk(j), :], coarse[...], preferred_element_type=f32).astype(bf)
        out2(j).start()

    wide_ref[frows(my_lead), lanes(half * kpad, my_group)] = jnp.dot(
        xt[blk(me), :], coarse[...], preferred_element_type=f32
    ).astype(bf)
    spec_ref[mrows(my_lead), lanes(0, my_group)] = coarse[mrows(me), :]

    @pl.loop(1, gx)
    def _(t):
        out3(lax.rem(me + t, gx)).start()

    forward(me, half).start()

    @pl.loop(1, gx)
    def _(t):
        f = lax.rem(my_lead + lead - t // groups, lead)
        g = lax.rem(my_group + t, groups)
        j = g * lead + f
        in2(j).wait_recv()
        forward(j, half).start()

    @pl.loop(0, lead)
    def _(f):
        swap(f).wait_send()

    @pl.loop(1, gx)
    def _(t):
        j = lax.rem(me + t, gx)
        in3(j).wait_recv()
        out1(j).wait_send()
        out2(j).wait_send()
        out3(j).wait_send()

    @pl.loop(0, gx)
    def _(j):
        forward(j, peer).wait_recv()
        forward(j, half).wait_send()


def exchange(gx, lead, x_local, kx, kpad, cols, grid, y_tab, x_parts):
    bf, f32 = jnp.bfloat16, jnp.float32
    rows, codes = lead * x_local, gx * kx
    dma = pltpu.SemaphoreType.DMA
    vmem = pl.BlockSpec(memory_space=pltpu.VMEM)
    return pl.pallas_call(
        functools.partial(exchange_kernel, gx, lead, x_local, kx, kpad, cols),
        out_shape=(
            jax.ShapeDtypeStruct((lead * kx, kpad), bf),
            jax.ShapeDtypeStruct((rows, 2 * kpad), bf),
        ),
        in_specs=[vmem] * 6,
        out_specs=(vmem, vmem),
        scratch_shapes=[
            pltpu.VMEM((rows, kpad), bf),
            pltpu.VMEM((rows, kpad), bf),
            pltpu.VMEM((rows, kpad), bf),
            pltpu.VMEM((gx * x_local, cols), bf),
            pltpu.VMEM((gx * x_local, codes), bf),
            pltpu.VMEM((cols, codes), f32),
            pltpu.VMEM((codes, cols), bf),
            pltpu.VMEM((gx * x_local, cols), bf),
            dma((lead,)), dma((lead,)),
        ] + [dma((gx,))] * 8,
        compiler_params=pltpu.CompilerParams(
            collective_id=0, has_side_effects=True, vmem_limit_bytes=48 * 1024 * 1024
        ),
    )(grid, y_tab, *x_parts)


def build(gx, gy):
    def local(fields, x_codes, y_codes):
        nf, nz, x_local, y_local = fields.shape
        lead = nf * nz
        ky = y_codes.shape[0] // gy
        kx = x_codes.shape[0] // gx
        unit = 128 * gx // math.gcd(128 * gx, lead)
        if unit > 2 * ky:
            unit = gx // math.gcd(gx, lead)
        kpad = -(-ky // unit) * unit
        cols = lead * kpad // gx
        me_y = lax.axis_index("gy")
        y_first = me_y * y_local
        padded = jnp.pad(y_codes.reshape(gy, ky), ((0, 0), (0, kpad - ky)))
        live = jnp.broadcast_to(jnp.arange(kpad)[None] < ky, (gy, kpad)).reshape(-1)
        y_tab = mode_table(padded.reshape(-1), y_first, y_local, NY, live)
        grid = fields.reshape(lead * x_local, y_local)
        if gy == 2 and cols % 128 == 0 and cols <= kpad and kpad // cols == gx // lead and x_local % 64 == 0 and kx % 16 == 0:
            x_parts = mode_parts(x_codes, 0, x_local * gx, NX)
            spec, wide = exchange(gx, lead, x_local, kx, kpad, cols, grid, y_tab, x_parts)
            low = lax.dot_general(wide, y_tab, (((1,), (1,)), ((), ())), preferred_element_type=jnp.float32)
            spectrum = spec.astype(jnp.float32)[:, :ky].reshape(nf, nz, kx, ky)
            return spectrum, low.reshape(nf, nz, x_local, y_local)
        x_tab = mode_table(x_codes, 0, x_local * gx, NX)
        part = jnp.dot(grid, y_tab, preferred_element_type=jnp.float32).reshape(lead * x_local, gy, kpad)
        own = lax.dynamic_index_in_dim(part, me_y, 1, keepdims=False)
        for shift in range(1, gy):
            there = lax.rem(me_y + shift, gy)
            block = lax.dynamic_index_in_dim(part, there, 1, keepdims=False).astype(jnp.bfloat16)
            got = lax.ppermute(block, "gy", [(i, (i + shift) % gy) for i in range(gy)])
            own = own + got.astype(jnp.float32)
        send = own.astype(jnp.bfloat16).reshape(lead, x_local, kpad)
        if cols <= kpad:
            def spread(a):
                n = a.shape[1]
                return a.reshape(lead, n, kpad // cols, cols).transpose(0, 2, 1, 3).reshape(gx, n, cols)

            def merge(a):
                n = a.shape[1]
                return a.reshape(lead, kpad // cols, n, cols).transpose(0, 2, 1, 3).reshape(lead, n, kpad)
        else:
            def spread(a):
                n = a.shape[1]
                return a.transpose(1, 0, 2).reshape(n, gx, cols).transpose(1, 0, 2)

            def merge(a):
                n = a.shape[1]
                return a.transpose(1, 0, 2).reshape(n, lead, kpad).transpose(1, 0, 2)
        lines = lax.all_to_all(spread(send), "gx", split_axis=0, concat_axis=0, tiled=True)
        lines = lines.reshape(gx * x_local, cols)
        modes = lax.dot_general(x_tab, lines, (((0,), (0,)), ((), ())), preferred_element_type=jnp.float32)
        coarse = modes.astype(jnp.bfloat16)
        synth = jnp.dot(x_tab, coarse, preferred_element_type=jnp.float32).astype(jnp.bfloat16)
        back = lax.all_to_all(synth.reshape(gx, x_local, cols), "gx", split_axis=0, concat_axis=0, tiled=True)
        spec = lax.all_to_all(coarse.reshape(gx, kx, cols), "gx", split_axis=0, concat_axis=0, tiled=True)
        spectrum = merge(spec)[:, :, :ky].astype(jnp.float32).reshape(nf, nz, kx, ky)
        mine = merge(back).reshape(lead * x_local, kpad)
        y_parts = y_tab.reshape(y_local, gy, kpad)
        whole = jnp.zeros((gy, lead * x_local, kpad), jnp.bfloat16)
        whole = lax.dynamic_update_index_in_dim(whole, mine, me_y, 0)
        for shift in range(1, gy):
            got = lax.ppermute(mine, "gy", [(i, (i + shift) % gy) for i in range(gy)])
            whole = lax.dynamic_update_index_in_dim(whole, got, lax.rem(me_y + gy - shift, gy), 0)
        wide = whole.transpose(1, 0, 2).reshape(lead * x_local, gy * kpad)
        low = lax.dot_general(wide, y_tab, (((1,), (1,)), ((), ())), preferred_element_type=jnp.float32)
        return spectrum, low.reshape(nf, nz, x_local, y_local)

    return local


def solution(mesh):
    return jax.shard_map(
        build(mesh.shape["gx"], mesh.shape["gy"]),
        mesh=mesh,
        in_specs=(P(None, None, "gx", "gy"), P(), P()),
        out_specs=(P(None, None, "gx", "gy"), P(None, None, "gx", "gy")),
        check_vma=False,
    )
```

profile of v0, /device:TPU:0, one launch (start us, length us, event | category | flops | bytes accessed | tf_op | source)
XLA Modules:
  0.0 70.0 jit_solution(12161344630618706793)
XLA Ops:
  0.6 0.0 copy-start
  0.7 0.8 %broadcast_compare_fusion = pred[1024]{0:T(1024)(128)(4,1)S(1)} fusion(s32[1024]{0:T(1024)} %param.4), kind=kLoop, calls=%fused_computation.48 | loop fusion | flops 1024 | bytes 5120 | tf_op jit(solution)/shard_map/le | solution.py:29
  1.5 0.7 add_select_fusion.4
  2.2 0.8 %reshape.103 = s32[2,510]{1,0:T(2,128)S(1)} reshape(s32[1020]{0:T(1024)} %param.5) | data formatting | bytes 8160 | tf_op jit(solution)/shard_map/reshape | solution.py:268
  3.1 0.7 compare_select_fusion
  3.7 0.5 select_multiply_fusion.2
  4.2 0.9 %select_multiply_fusion = (f32[48,1024]{1,0:T(8,128)S(1)}, f32[48,1024]{1,0:T(8,128)S(1)}) fusion(f32[1024]{0:T(1024)S(1)} %compare_select_fusion, s32[48]{0:T(128)S(1)} %iota_multiply_fusion, s32[1024]{0:T(1024)S(1)} %add_select_fusion.4, pred[1024]{0:T(1024)(128)(4,1)S(1)} %broadcast_compare_fusion), kind=kLoop, calls=%fused_computation.23 | loop fusion | flops 688128 | bytes 402624 | tf_op jit(solution)/shard_map/mul | solution.py:32
  5.2 1.1 %fusion.6 = (f32[64,1024]{1,0:T(8,128)S(1)}, f32[64,1024]{1,0:T(8,128)S(1)}) fusion(s32[1024]{0:T(1024)S(1)} %add_select_fusion.4), kind=kLoop, calls=%fused_computation.12 | loop fusion | flops 589824 | bytes 528384 | tf_op jit(solution)/shard_map/sin | solution.py:33
  6.2 1.1 %fusion.10 = (f32[64,1024]{1,0:T(8,128)S(1)}, f32[64,1024]{1,0:T(8,128)S(1)}) fusion(s32[1024]{0:T(1024)S(1)} %add_select_fusion.5), kind=kLoop, calls=%fused_computation.17 | loop fusion | flops 589824 | bytes 528384 | tf_op jit(solution)/shard_map/sin | solution.py:33
  7.3 2.6 %add_convert_fusion = bf16[24,64,1024]{2,1,0:T(8,128)(2,1)} fusion(f32[64,1024]{1,0:T(8,128)S(1)} %get-tuple-element.15, f32[24,1024]{1,0:T(8,128)S(1)} %get-tuple-element.14, f32[64,1024]{1,0:T(8,128)S(1)} %get-tuple-element.13, f32[24,1024]{1,0:T(8,128)S(1)} %get-tuple-element.12), kind=kLoop, calls=%fused_computation | loop fusion | flops 6291456 | bytes 3866624 | tf_op jit(solution)/shard_map/convert_element_type | solution.py:40
  9.9 0.0 copy-done
  9.9 0.0 copy-start.1
  9.9 54.9 %shard_map.50 = (bf16[256,512]{1,0:T(8,128)(2,1)S(1)}, bf16[768,1024]{1,0:T(8,128)(2,1)S(1)}) custom-call(bf16[768,1536]{1,0:T(8,128)(2,1)S(1)} %bitcast.20, bf16[1536,1024]{1,0:T(8,128)(2,1)} %bitcast.23, f32[48,1024]{1,0:T(8,128)S(1)} %get-tuple-element.16.xa_ref, f32[48,1024]{1,0:T(8,128)S(1)} %get-tuple-element.17.xb_ref, ...), custom_call_target="tpu_custom_call" | custom-call | tf_op jit(solution)/shard_map/pallas_call | solution.py:230
  64.8 0.0 copy-done.1
  64.8 4.3 %convolution_bitcast_fusion = f32[4,1,192,1536]{3,2,1,0:T(8,128)} fusion(bf16[4,192,1024]{2,1,0:T(8,128)(2,1)S(1)} %bitcast.22, bf16[1536,1024,1]{1,0,2:T(8,128)(2,1)S(1)} %bitcast.24), kind=kOutput, calls=%fused_computation.1 | convolution fusion | flops 2415919104 | bytes 9437184 | tf_op jit(solution)/shard_map/dot_general | solution.py:275
  69.1 0.9 %convert.3 = f32[4,1,64,510]{3,2,1,0:T(8,128)} convert(bf16[4,1,64,510]{3,2,1,0:T(8,128)(2,1)S(1)} %bitcast.21) | non-fusion elementwise | flops 130560 | bytes 783360
  (10 shorter events, 0.1 us)
Async XLA Ops:
  0.6 9.3 %copy-start = (bf16[4,1,192,1536]{3,2,1,0:T(8,128)(2,1)S(1)}, bf16[4,1,192,1536]{3,2,1,0:T(8,128)(2,1)}, u32[]{:S(2)}) copy-start(bf16[4,1,192,1536]{3,2,1,0:T(8,128)(2,1)} %param.3) | copy-start | bytes 7077892
  9.9 54.9 %copy-start.1 = (bf16[24,64,1024]{2,1,0:T(8,128)(2,1)S(1)}, bf16[24,64,1024]{2,1,0:T(8,128)(2,1)}, u32[]{:S(2)}) copy-start(bf16[24,64,1024]{2,1,0:T(8,128)(2,1)} %add_convert_fusion) | copy-start | bytes 9437188
where the time goes:
time: 70.3 us; the launch traced here: 70 us
  Pallas kernels  54.9 us (78%)
  other arithmetic  9.24 us (13%)
  matrix products  4.29 us (6%)
  local copies, waits for them, and re-layouts  0.81 us (1%)
  between operations  0.72 us (1%)
    pallas_call x1, Pallas kernels, exchange(): pl.pallas_call(functools.partial(exchange_kernel, gx, lead, x_local, kx,...  54.9 us
    dot_general x1, matrix products, local(): lax.dot_general(wide, y_tab, (((1,), (1,)), ((), ())), preferred_element_...  4.29 us
    convert_element_type x1, other arithmetic, mode_table(): return table.astype(jnp.bfloat16).reshape(amount, picked.shape[0])  2.58 us
    sin x2, other arithmetic, mode_parts(): fc, fs = (jnp.cos(fine_angle), jnp.sin(fine_angle))  2.14 us

commit v1 on v0

--- a/solution.py
+++ b/solution.py
@@ -11,6 +11,7 @@
 NX = 3072
 NY = 3072
 BAND = 512
+STEP = 64
 
 
 def angle(freq, position, length):
@@ -44,11 +45,55 @@
     return pl.multiple_of(v, m)
 
 
+def turn(freq, position, shift, length):
+    product = freq * position
+    quarter = jnp.floor(product * (4.0 / length) + 0.5)
+    x = (product * 4.0 - quarter * length) * (2.0 * math.pi / (4 * length))
+    x2 = x * x
+    s = x + x * x2 * (-1 / 6 + x2 * (1 / 120 + x2 * (-1 / 5040 + x2 * (1 / 362880))))
+    c = 1.0 + x2 * (-0.5 + x2 * (1 / 24 + x2 * (-1 / 720 + x2 * (1 / 40320))))
+    quarter = quarter - shift
+    q = quarter - 4.0 * jnp.floor(quarter * 0.25)
+    odd = (q == 1.0) | (q == 3.0)
+    cos_value, sin_value = jnp.where(odd, s, c), jnp.where(odd, c, s)
+    cos_value = jnp.where((q == 1.0) | (q == 2.0), -cos_value, cos_value)
+    return cos_value, jnp.where(q >= 2.0, -sin_value, sin_value)
+
+
+def make_table(code_ref, first, length, table, ta, tb, fc, fs):
+    amount, codes = table.shape
+    f32 = jnp.float32
+    code = code_ref[...]
+    freq = jnp.where(code <= BAND, code, code - BAND).astype(f32)
+    shift = jnp.where(code <= BAND, 0, 1).astype(f32)
+    norm = jnp.where(code == 0, 1.0 / math.sqrt(length), math.sqrt(2.0 / length)).astype(f32)
+    norm = jnp.where(code < 0, 0.0, norm)
+    row = lax.broadcasted_iota(jnp.int32, (8, codes), 0)
+
+    @pl.loop(0, amount // STEP // 8)
+    def _(i):
+        c, s = turn(freq, (first + (row + i * 8) * STEP).astype(f32), shift, length)
+        ta[pl.ds(al(i * 8, 8), 8), :] = c * norm
+        tb[pl.ds(al(i * 8, 8), 8), :] = s * norm
+
+    @pl.loop(0, STEP // 8)
+    def _(i):
+        c, s = turn(freq, (row + i * 8).astype(f32), 0.0, length)
+        fc[pl.ds(al(i * 8, 8), 8), :] = c
+        fs[pl.ds(al(i * 8, 8), 8), :] = s
+
+    @pl.loop(0, amount // STEP)
+    def _(h):
+        table[pl.ds(al(h * STEP, STEP), STEP), :] = (
+            ta[pl.ds(h, 1), :] * fc[...] - tb[pl.ds(h, 1), :] * fs[...]
+        ).astype(jnp.bfloat16)
+
+
 def exchange_kernel(
     gx, lead, x_local, kx, kpad, cols,
-    grid_ref, y_ref, xa_ref, xb_ref, fc_ref, fs_ref, spec_ref, wide_ref,
-    other, inc, part, lines, xt, acc, coarse, syn,
-    gs, gr, s1, r1, s2, r2, s3, r3, s4, r4,
+    grid_ref, xcode_ref, ycode_ref, spec_ref, wide_ref, y_out,
+    y_ref, ta, tb, fc, fs, other, inc, part, lines, xt, acc, coarse, syn,
+    gs, gr, s1, r1, s2, r2, s3, r3, s4, r4, y_sem,
 ):
     me = lax.axis_index("gx")
     half = lax.axis_index("gy")
@@ -73,6 +118,10 @@
     def lanes(base, g):
         return pl.ds(al(base + g * cols, cols), cols)
 
+    make_table(ycode_ref, half * y_ref.shape[0], NY, y_ref, ta, tb, fc, fs)
+    y_copy = pltpu.make_async_copy(y_ref, y_out, y_sem)
+    y_copy.start()
+
     @pl.loop(0, lead)
     def _(t):
         f = lax.rem(my_lead + t, lead)
@@ -122,14 +171,7 @@
 
     lines[blk(me), :] = part[frows(my_lead), lanes(0, my_group)]
 
-    step = fc_ref.shape[0]
-
-    @pl.loop(0, xa_ref.shape[0])
-    def _(h):
-        xt[pl.ds(al(h * step, step), step), :] = (
-            xa_ref[pl.ds(h, 1), :] * fc_ref[...] + xb_ref[pl.ds(h, 1), :] * fs_ref[...]
-        ).astype(bf)
-
+    make_table(xcode_ref, 0, NX, xt, ta, tb, fc, fs)
     acc[...] = jnp.zeros_like(acc)
 
     @pl.loop(0, gx)
@@ -204,6 +246,8 @@
         in2(j).wait_recv()
         forward(j, half).start()
 
+    y_copy.wait()
+
     @pl.loop(0, lead)
     def _(f):
         swap(f).wait_send()
@@ -222,20 +266,28 @@
         forward(j, half).wait_send()
 
 
-def exchange(gx, lead, x_local, kx, kpad, cols, grid, y_tab, x_parts):
+def exchange(gx, lead, x_local, kx, kpad, cols, grid, x_codes, y_codes):
     bf, f32 = jnp.bfloat16, jnp.float32
     rows, codes = lead * x_local, gx * kx
     dma = pltpu.SemaphoreType.DMA
     vmem = pl.BlockSpec(memory_space=pltpu.VMEM)
+    y_local = grid.shape[1]
+    tall = max(gx * x_local, y_local) // STEP
     return pl.pallas_call(
         functools.partial(exchange_kernel, gx, lead, x_local, kx, kpad, cols),
         out_shape=(
             jax.ShapeDtypeStruct((lead * kx, kpad), bf),
             jax.ShapeDtypeStruct((rows, 2 * kpad), bf),
+            jax.ShapeDtypeStruct((y_local, 2 * kpad), bf),
         ),
-        in_specs=[vmem] * 6,
-        out_specs=(vmem, vmem),
+        in_specs=[vmem] * 3,
+        out_specs=(vmem, vmem, pl.BlockSpec(memory_space=pl.ANY)),
         scratch_shapes=[
+            pltpu.VMEM((y_local, 2 * kpad), bf),
+            pltpu.VMEM((tall, codes), f32),
+            pltpu.VMEM((tall, codes), f32),
+            pltpu.VMEM((STEP, codes), f32),
+            pltpu.VMEM((STEP, codes), f32),
             pltpu.VMEM((rows, kpad), bf),
             pltpu.VMEM((rows, kpad), bf),
             pltpu.VMEM((rows, kpad), bf),
@@ -245,11 +297,11 @@
             pltpu.VMEM((codes, cols), bf),
             pltpu.VMEM((gx * x_local, cols), bf),
             dma((lead,)), dma((lead,)),
-        ] + [dma((gx,))] * 8,
+        ] + [dma((gx,))] * 8 + [dma],
         compiler_params=pltpu.CompilerParams(
             collective_id=0, has_side_effects=True, vmem_limit_bytes=48 * 1024 * 1024
         ),
-    )(grid, y_tab, *x_parts)
+    )(grid, x_codes, y_codes)
 
 
 def build(gx, gy):
@@ -269,9 +321,11 @@
         live = jnp.broadcast_to(jnp.arange(kpad)[None] < ky, (gy, kpad)).reshape(-1)
         y_tab = mode_table(padded.reshape(-1), y_first, y_local, NY, live)
         grid = fields.reshape(lead * x_local, y_local)
-        if gy == 2 and cols % 128 == 0 and cols <= kpad and kpad // cols == gx // lead and x_local % 64 == 0 and kx % 16 == 0:
-            x_parts = mode_parts(x_codes, 0, x_local * gx, NX)
-            spec, wide = exchange(gx, lead, x_local, kx, kpad, cols, grid, y_tab, x_parts)
+        if gy == 2 and cols % 128 == 0 and cols <= kpad and kpad // cols == gx // lead and x_local % (8 * STEP // gx) == 0 and y_local % (8 * STEP) == 0 and kx % 16 == 0 and gx * kx == gy * kpad:
+            padded = jnp.pad(y_codes.reshape(gy, ky), ((0, 0), (0, kpad - ky)), constant_values=-1)
+            spec, wide, y_tab = exchange(
+                gx, lead, x_local, kx, kpad, cols, grid, x_codes.reshape(1, -1), padded.reshape(1, -1)
+            )
             low = lax.dot_general(wide, y_tab, (((1,), (1,)), ((), ())), preferred_element_type=jnp.float32)
             spectrum = spec.astype(jnp.float32)[:, :ky].reshape(nf, nz, kx, ky)
             return spectrum, low.reshape(nf, nz, x_local, y_local)

time: 70.3 us -> 63.8 us (0.908)
  other arithmetic: 9.24 us -> 0.85 us
  local copies, waits for them, and re-layouts: 0.81 us -> 3.13 us
  Pallas kernels: 54.9 us -> 52.7 us
  matrix products: 4.29 us -> 6.17 us
    convert_element_type x1 -> x0, other arithmetic: 2.58 us -> none  [mode_table(): return table.astype(jnp.bfloat16).reshape(amount, picked.shape[0])]
    unnamed x6, local copies, waits for them, and re-layouts: 0.02 us -> 2.36 us
    pallas_call x1, Pallas kernels: 54.9 us -> 52.7 us  [exchange(): pl.pallas_call(functools.partial(exchange_kernel, gx, lead, x_local, kx,...]
    sin x2 -> x0, other arithmetic: 2.14 us -> none  [mode_parts(): fc, fs = (jnp.cos(fine_angle), jnp.sin(fine_angle))]
    dot_general x1, matrix products: 4.29 us -> 6.17 us  [local(): lax.dot_general(wide, y_tab, (((1,), (1,)), ((), ())), preferred_element_...]
    mul x3 -> x0, other arithmetic: 1.41 us -> none  [the longest x2 1.4 us: mode_parts(): second_part = jnp.where(is_cos, -s, c) * norm[None, :]]
    select_n x4 -> x0, other arithmetic: 1.39 us -> none  [the longest x2 0.69 us: mode_parts(): freq = jnp.where(picked <= BAND, picked, picked - BAND)]
    le x2 -> x0, other arithmetic: 0.85 us -> none  [mode_parts(): is_cos = (picked <= BAND)[None, :]]
where the time goes in v1:
time: 63.8 us; the launch traced here: 63.5 us
  Pallas kernels  52.7 us (83%)
  matrix products  6.17 us (10%)
  local copies, waits for them, and re-layouts  3.13 us (5%)
  other arithmetic  0.85 us (1%)
  between operations  0.65 us (1%)
    pallas_call x1, Pallas kernels, exchange(): pl.pallas_call(functools.partial(exchange_kernel, gx, lead, x_local, kx,...  52.7 us
    dot_general x1, matrix products, local(): lax.dot_general(wide, y_tab, (((1,), (1,)), ((), ())), preferred_element_...  6.17 us
    unnamed x6, local copies, waits for them, and re-layouts  2.36 us

profile of v1, /device:TPU:0, one launch (start us, length us, event | category | flops | bytes accessed | tf_op | source)
XLA Modules:
  0.0 63.5 jit_solution(11583410960210822954)
XLA Ops:
  0.6 0.8 %reshape.27 = s32[2,510]{1,0:T(2,128)S(1)} reshape(s32[1020]{0:T(1024)} %param.5) | data formatting | bytes 8160 | tf_op jit(solution)/shard_map/reshape | solution.py:325
  1.4 0.0 copy-start
  1.4 1.7 %copy-done = bf16[4,1,192,1536]{3,2,1,0:T(8,128)(2,1)S(1)} copy-done((bf16[4,1,192,1536]{3,2,1,0:T(8,128)(2,1)S(1)}, bf16[4,1,192,1536]{3,2,1,0:T(8,128)(2,1)}, u32[]{:S(2)}) %copy-start) | copy-done | bytes 2359320
  3.1 0.0 copy-start.1
  3.1 0.7 %copy-done.1 = s32[1024]{0:T(1024)S(1)} copy-done((s32[1024]{0:T(1024)S(1)}, s32[1024]{0:T(1024)}, u32[]{:S(2)}) %copy-start.1) | copy-done | bytes 4120
  3.8 52.7 %shard_map.50 = (bf16[256,512]{1,0:T(8,128)(2,1)S(1)}, bf16[768,1024]{1,0:T(8,128)(2,1)S(1)}, bf16[1536,1024]{1,0:T(8,128)(2,1)}) custom-call(bf16[768,1536]{1,0:T(8,128)(2,1)S(1)} %bitcast.17, s32[1,1024]{1,0:T(1,128)S(1)} %bitcast.20, s32[1,1024]{1,0:T(1,128)S(1)} %bitcast.19), custom_call_target="tpu_custom_call" | custom-call | tf_op jit(solution)/shard_map/pallas_call | solution.py:276
  56.4 6.2 %fusion = f32[768,1536]{1,0:T(8,128)} fusion(bf16[768,1024]{1,0:T(8,128)(2,1)S(1)} %get-tuple-element.6, bf16[1536,1024]{1,0:T(8,128)(2,1)} %get-tuple-element.7), kind=kOutput, calls=%fused_computation.1 | convolution fusion | flops 2415919104 | bytes 9437184 | tf_op jit(solution)/shard_map/dot_general | solution.py:329
  62.6 0.9 %convert.3 = f32[4,1,64,510]{3,2,1,0:T(8,128)} convert(bf16[4,1,64,510]{3,2,1,0:T(8,128)(2,1)S(1)} %bitcast.18) | non-fusion elementwise | flops 130560 | bytes 783360
  (2 shorter events, 0.0 us)
Async XLA Ops:
  1.4 1.7 %copy-start = (bf16[4,1,192,1536]{3,2,1,0:T(8,128)(2,1)S(1)}, bf16[4,1,192,1536]{3,2,1,0:T(8,128)(2,1)}, u32[]{:S(2)}) copy-start(bf16[4,1,192,1536]{3,2,1,0:T(8,128)(2,1)} %param.3) | copy-start | bytes 7077892
  3.1 0.7 %copy-start.1 = (s32[1024]{0:T(1024)S(1)}, s32[1024]{0:T(1024)}, u32[]{:S(2)}) copy-start(s32[1024]{0:T(1024)} %param.4) | copy-start | bytes 12292

commit v2 on v1

--- a/solution.py
+++ b/solution.py
@@ -91,9 +91,9 @@
 
 def exchange_kernel(
     gx, lead, x_local, kx, kpad, cols,
-    grid_ref, xcode_ref, ycode_ref, spec_ref, wide_ref, y_out,
-    y_ref, ta, tb, fc, fs, other, inc, part, lines, xt, acc, coarse, syn,
-    gs, gr, s1, r1, s2, r2, s3, r3, s4, r4, y_sem,
+    grid_in, xcode_ref, ycode_ref, spec_ref, low_out,
+    grid_ref, wide_ref, low_ref, y_ref, ta, tb, fc, fs, other, inc, part, lines, xt, acc, coarse, syn,
+    gs, gr, s1, r1, s2, r2, s3, r3, s4, r4, grid_sem, low_sem,
 ):
     me = lax.axis_index("gx")
     half = lax.axis_index("gy")
@@ -102,6 +102,8 @@
     my_group, my_lead = me // lead, lax.rem(me, lead)
     bf, f32 = jnp.bfloat16, jnp.float32
 
+    grid_copy = pltpu.make_async_copy(grid_in, grid_ref, grid_sem)
+    grid_copy.start()
     barrier = pltpu.get_barrier_semaphore()
     pl.semaphore_signal(barrier, inc=1, device_id={"gy": peer})
 
@@ -119,8 +121,7 @@
         return pl.ds(al(base + g * cols, cols), cols)
 
     make_table(ycode_ref, half * y_ref.shape[0], NY, y_ref, ta, tb, fc, fs)
-    y_copy = pltpu.make_async_copy(y_ref, y_out, y_sem)
-    y_copy.start()
+    grid_copy.wait()
 
     @pl.loop(0, lead)
     def _(t):
@@ -238,19 +239,30 @@
 
     forward(me, half).start()
 
-    @pl.loop(1, gx)
-    def _(t):
-        f = lax.rem(my_lead + lead - t // groups, lead)
-        g = lax.rem(my_group + t, groups)
-        j = g * lead + f
-        in2(j).wait_recv()
-        forward(j, half).start()
-
-    y_copy.wait()
+    def low_copy(f):
+        return pltpu.make_async_copy(low_ref.at[frows(f), :], low_out.at[frows(f), :], low_sem.at[f])
 
     @pl.loop(0, lead)
-    def _(f):
-        swap(f).wait_send()
+    def _(t):
+        f = lax.rem(my_lead + lead - t, lead)
+
+        @pl.loop(0, groups)
+        def _(u):
+            j = lax.rem(my_group + u, groups) * lead + f
+
+            @pl.when(j != me)
+            def _():
+                in2(j).wait_recv()
+                forward(j, half).start()
+
+        @pl.loop(0, groups)
+        def _(u):
+            forward(u * lead + f, peer).wait_recv()
+
+        low_ref[frows(f), :] = lax.dot_general(
+            wide_ref[frows(f), :], y_ref[...], (((1,), (1,)), ((), ())), preferred_element_type=f32
+        ).astype(bf)
+        low_copy(f).start()
 
     @pl.loop(1, gx)
     def _(t):
@@ -262,8 +274,12 @@
 
     @pl.loop(0, gx)
     def _(j):
-        forward(j, peer).wait_recv()
         forward(j, half).wait_send()
+
+    @pl.loop(0, lead)
+    def _(f):
+        swap(f).wait_send()
+        low_copy(f).wait()
 
 
 def exchange(gx, lead, x_local, kx, kpad, cols, grid, x_codes, y_codes):
@@ -277,12 +293,14 @@
         functools.partial(exchange_kernel, gx, lead, x_local, kx, kpad, cols),
         out_shape=(
             jax.ShapeDtypeStruct((lead * kx, kpad), bf),
-            jax.ShapeDtypeStruct((rows, 2 * kpad), bf),
-            jax.ShapeDtypeStruct((y_local, 2 * kpad), bf),
+            jax.ShapeDtypeStruct((rows, y_local), bf),
         ),
-        in_specs=[vmem] * 3,
-        out_specs=(vmem, vmem, pl.BlockSpec(memory_space=pl.ANY)),
+        in_specs=[pl.BlockSpec(memory_space=pl.ANY), vmem, vmem],
+        out_specs=(vmem, pl.BlockSpec(memory_space=pl.ANY)),
         scratch_shapes=[
+            pltpu.VMEM((rows, y_local), bf),
+            pltpu.VMEM((rows, 2 * kpad), bf),
+            pltpu.VMEM((rows, y_local), bf),
             pltpu.VMEM((y_local, 2 * kpad), bf),
             pltpu.VMEM((tall, codes), f32),
             pltpu.VMEM((tall, codes), f32),
@@ -297,9 +315,9 @@
             pltpu.VMEM((codes, cols), bf),
             pltpu.VMEM((gx * x_local, cols), bf),
             dma((lead,)), dma((lead,)),
-        ] + [dma((gx,))] * 8 + [dma],
+        ] + [dma((gx,))] * 8 + [dma, dma((lead,))],
         compiler_params=pltpu.CompilerParams(
-            collective_id=0, has_side_effects=True, vmem_limit_bytes=48 * 1024 * 1024
+            collective_id=0, has_side_effects=True, vmem_limit_bytes=60 * 1024 * 1024
         ),
     )(grid, x_codes, y_codes)
 
@@ -319,17 +337,17 @@
         y_first = me_y * y_local
         padded = jnp.pad(y_codes.reshape(gy, ky), ((0, 0), (0, kpad - ky)))
         live = jnp.broadcast_to(jnp.arange(kpad)[None] < ky, (gy, kpad)).reshape(-1)
-        y_tab = mode_table(padded.reshape(-1), y_first, y_local, NY, live)
         grid = fields.reshape(lead * x_local, y_local)
         if gy == 2 and cols % 128 == 0 and cols <= kpad and kpad // cols == gx // lead and x_local % (8 * STEP // gx) == 0 and y_local % (8 * STEP) == 0 and kx % 16 == 0 and gx * kx == gy * kpad:
             padded = jnp.pad(y_codes.reshape(gy, ky), ((0, 0), (0, kpad - ky)), constant_values=-1)
-            spec, wide, y_tab = exchange(
+            spec, low = exchange(
                 gx, lead, x_local, kx, kpad, cols, grid, x_codes.reshape(1, -1), padded.reshape(1, -1)
             )
-            low = lax.dot_general(wide, y_tab, (((1,), (1,)), ((), ())), preferred_element_type=jnp.float32)
+            low = low.astype(jnp.float32)
             spectrum = spec.astype(jnp.float32)[:, :ky].reshape(nf, nz, kx, ky)
             return spectrum, low.reshape(nf, nz, x_local, y_local)
         x_tab = mode_table(x_codes, 0, x_local * gx, NX)
+        y_tab = mode_table(padded.reshape(-1), y_first, y_local, NY, live)
         part = jnp.dot(grid, y_tab, preferred_element_type=jnp.float32).reshape(lead * x_local, gy, kpad)
         own = lax.dynamic_index_in_dim(part, me_y, 1, keepdims=False)
         for shift in range(1, gy):

time: 63.8 us -> 63 us (0.987); the launches traced: 63.5 us -> 61.8 us
  matrix products: 6.17 us -> 0 us
  other arithmetic: 0.85 us -> 5.39 us
  local copies, waits for them, and re-layouts: 3.13 us -> 1.38 us
  Pallas kernels: 52.7 us -> 54.4 us
    dot_general x1 -> x0, matrix products: 6.17 us -> none  [local(): lax.dot_general(wide, y_tab, (((1,), (1,)), ((), ())), preferred_element_...]
    unnamed x1 -> x2, other arithmetic: 0.85 us -> 5.39 us
    unnamed x6 -> x4, local copies, waits for them, and re-layouts: 2.36 us -> 0.61 us
    pallas_call x1, Pallas kernels: 52.7 us -> 54.4 us  [exchange(): pl.pallas_call(functools.partial(exchange_kernel, gx, lead, x_local, kx,...]
where the time goes in v2:
time: 63 us; the launch traced here: 61.8 us
  Pallas kernels  54.4 us (86%)
  other arithmetic  5.39 us (9%)
  local copies, waits for them, and re-layouts  1.38 us (2%)
  between operations  0.65 us (1%)
    pallas_call x1, Pallas kernels, exchange(): pl.pallas_call(functools.partial(exchange_kernel, gx, lead, x_local, kx,...  54.4 us
    unnamed x2, other arithmetic  5.39 us

profile of v2, /device:TPU:0, one launch (start us, length us, event | category | flops | bytes accessed | tf_op | source)
XLA Modules:
  0.0 61.8 jit_solution(9767326592186261480)
XLA Ops:
  0.6 0.8 %reshape.30 = s32[2,510]{1,0:T(2,128)S(1)} reshape(s32[1020]{0:T(1024)} %param.5) | data formatting | bytes 8160 | tf_op jit(solution)/shard_map/reshape | solution.py:342
  1.4 0.6 copy.7
  2.0 54.4 %shard_map.50 = (bf16[256,512]{1,0:T(8,128)(2,1)}, bf16[768,1536]{1,0:T(8,128)(2,1)}) custom-call(bf16[768,1536]{1,0:T(8,128)(2,1)} %bitcast.18, s32[1,1024]{1,0:T(1,128)} %bitcast.21, s32[1,1024]{1,0:T(1,128)} %bitcast.20), custom_call_target="tpu_custom_call" | custom-call | tf_op jit(solution)/shard_map/pallas_call | solution.py:292
  56.4 0.0 copy-start
  56.4 4.5 %convert.6 = f32[4,1,192,1536]{3,2,1,0:T(8,128)} convert(bf16[4,1,192,1536]{3,2,1,0:T(8,128)(2,1)} %bitcast.17) | non-fusion elementwise | flops 1179648 | bytes 7077888
  60.9 0.0 copy-done
  60.9 0.9 %convert.4 = f32[4,1,64,510]{3,2,1,0:T(8,128)} convert(bf16[4,1,64,510]{3,2,1,0:T(8,128)(2,1)S(1)} %bitcast.19) | non-fusion elementwise | flops 130560 | bytes 783360
  (1 shorter events, 0.0 us)
Async XLA Ops:
  56.4 4.5 %copy-start = (bf16[256,512]{1,0:T(8,128)(2,1)S(1)}, bf16[256,512]{1,0:T(8,128)(2,1)}, u32[]{:S(2)}) copy-start(bf16[256,512]{1,0:T(8,128)(2,1)} %get-tuple-element.4) | copy-start | bytes 786436

commit v3 on v2

--- a/solution.py
+++ b/solution.py
@@ -120,7 +120,12 @@
     def lanes(base, g):
         return pl.ds(al(base + g * cols, cols), cols)
 
-    make_table(ycode_ref, half * y_ref.shape[0], NY, y_ref, ta, tb, fc, fs)
+    def y_half(side):
+        span = pl.ds(al(side * kpad, kpad), kpad)
+        narrow = [r.at[:, pl.ds(0, kpad)] for r in (ta, tb, fc, fs)]
+        make_table(ycode_ref.at[:, span], half * y_ref.shape[0], NY, y_ref.at[:, span], *narrow)
+
+    y_half(peer)
     grid_copy.wait()
 
     @pl.loop(0, lead)
@@ -140,6 +145,8 @@
     @pl.loop(0, lead)
     def _(t):
         swap(lax.rem(my_lead + t, lead)).start()
+
+    y_half(half)
 
     def out1(j):
         f, g = lax.rem(j, lead), j // lead

time: 63 us -> 63.1 us (level); the launches traced: 61.8 us -> 62.7 us
  Pallas kernels: 54.4 us -> 55.2 us
    pallas_call x1, Pallas kernels: 54.4 us -> 55.2 us  [exchange(): pl.pallas_call(functools.partial(exchange_kernel, gx, lead, x_local, kx,...]
where the time goes in v3:
time: 63.1 us; the launch traced here: 62.7 us
  Pallas kernels  55.2 us (87%)
  other arithmetic  5.39 us (9%)
  local copies, waits for them, and re-layouts  1.38 us (2%)
  between operations  0.65 us (1%)
    pallas_call x1, Pallas kernels, exchange(): pl.pallas_call(functools.partial(exchange_kernel, gx, lead, x_local, kx,...  55.2 us
    unnamed x2, other arithmetic  5.39 us

profile of v3, /device:TPU:0, one launch (start us, length us, event | category | flops | bytes accessed | tf_op | source)
XLA Modules:
  0.0 62.7 jit_solution(9512221431507723799)
XLA Ops:
  0.6 0.8 %reshape.30 = s32[2,510]{1,0:T(2,128)S(1)} reshape(s32[1020]{0:T(1024)} %param.5) | data formatting | bytes 8160 | tf_op jit(solution)/shard_map/reshape | solution.py:349
  1.4 0.6 copy.7
  2.0 55.2 %shard_map.50 = (bf16[256,512]{1,0:T(8,128)(2,1)}, bf16[768,1536]{1,0:T(8,128)(2,1)}) custom-call(bf16[768,1536]{1,0:T(8,128)(2,1)} %bitcast.18, s32[1,1024]{1,0:T(1,128)} %bitcast.21, s32[1,1024]{1,0:T(1,128)} %bitcast.20), custom_call_target="tpu_custom_call" | custom-call | tf_op jit(solution)/shard_map/pallas_call | solution.py:299
  57.3 0.0 copy-start
  57.3 4.5 %convert.6 = f32[4,1,192,1536]{3,2,1,0:T(8,128)} convert(bf16[4,1,192,1536]{3,2,1,0:T(8,128)(2,1)} %bitcast.17) | non-fusion elementwise | flops 1179648 | bytes 7077888
  61.8 0.0 copy-done
  61.8 0.9 %convert.4 = f32[4,1,64,510]{3,2,1,0:T(8,128)} convert(bf16[4,1,64,510]{3,2,1,0:T(8,128)(2,1)S(1)} %bitcast.19) | non-fusion elementwise | flops 130560 | bytes 783360
  (1 shorter events, 0.0 us)
Async XLA Ops:
  57.3 4.5 %copy-start = (bf16[256,512]{1,0:T(8,128)(2,1)S(1)}, bf16[256,512]{1,0:T(8,128)(2,1)}, u32[]{:S(2)}) copy-start(bf16[256,512]{1,0:T(8,128)(2,1)} %get-tuple-element.4) | copy-start | bytes 786436
